TPU v7x, 32 devices: a whole 2x2x4 slice. The times are simulated.
32 devices in a mesh: dp: 4 (over x, core), pipe: 4 (over z), tensor: 2 (over y).
Axes of the slice: x: 2, y: 2, z: 4, core: 2. Of those that a mesh axis runs over, the one named last changes fastest.
Arguments:
- support_tokens: int32 [32, 32], P(('dp', 'pipe')), may hold values from 0 to 64127
- support_lengths: int32 [32], P(('dp', 'pipe')), may hold values from 1 to 32
- support_labels: int32 [32, 1], P(('dp', 'pipe')), may hold values from 0 to 31
- query_tokens: int32 [16, 32], P(('dp', 'pipe')), may hold values from 0 to 64127
- query_lengths: int32 [16], P(('dp', 'pipe')), may hold values from 1 to 32
- query_episodes: int32 [16], P(('dp', 'pipe')), may hold values from 0 to 1
- embedding: bfloat16 [64128, 4096], P(('dp', 'pipe'), 'tensor'), may hold values from -18 to 18
- attn_gain: float32 [4, 4096], P('pipe'), may hold values from 0.5 to 1.5
- query_weight: bfloat16 [4, 4096, 4096], P('pipe', None, 'tensor'), may hold values from -1 to 1
- key_weight: bfloat16 [4, 4096, 1024], P('pipe', None, 'tensor'), may hold values from -16 to 16
- value_weight: bfloat16 [4, 4096, 1024], P('pipe', None, 'tensor'), may hold values from -0.09375 to 0.09375
- out_weight: bfloat16 [4, 4096, 4096], P('pipe', 'tensor'), may hold values from -0.09375 to 0.09375
- final_gain: float32 [4096], replicated, may hold values from 0.5 to 1.5
Outputs:
- prototypes: float32 [32, 4096], P(None, 'tensor')
- logits: float32 [16, 16], P(('dp', 'pipe'))
Inputs may be any that keep to these rules, and one draw needn't show every extreme that they name: `support_labels`: every class is the label of at least one support sequence.
All inputs are finite; a program needn't handle non-finite values.
Results may differ from a plain program's by a relative error of at most 0.024.
Values may be sent and summed in bfloat16 or wider, within the bound.
No kernel may reach another device: no remote copies, remote signals or barrier semaphores. Data moves between devices by JAX's collectives and lax.ppermute only.
A program may use at most 128 MiB of HBM per device.

v0:
```python
import math
import jax
import jax.numpy as jnp
from jax import lax
from jax.sharding import PartitionSpec as P

D = 4096
HEAD_DIM = 128
WAYS = 16
EPISODES = 2
epsilon = 1e-05
rotary_base = 500000.0


def passed_along(block, axis, distance):
    devices = range(lax.axis_size(axis))
    route = [((i - distance) % len(devices), i) for i in devices]
    return lax.ppermute(block, axis, route)


def rotate(heads_in, seq_len):
    half_dim = HEAD_DIM // 2
    freqs = jnp.exp(
        -math.log(rotary_base) * jnp.arange(half_dim, dtype=jnp.float32) * (2.0 / HEAD_DIM)
    )
    angles = jnp.arange(seq_len, dtype=jnp.float32)[:, None] * freqs[None, :]
    cosine = jnp.cos(angles)[None, :, None, :]
    sine = jnp.sin(angles)[None, :, None, :]
    first_half = heads_in[..., :half_dim]
    second_half = heads_in[..., half_dim:]
    return jnp.concatenate(
        [first_half * cosine - second_half * sine, second_half * cosine + first_half * sine],
        axis=-1,
    )


def whole_rows(hidden):
    return lax.all_gather(hidden, "tensor", axis=1, tiled=True)


def whole_values(full_rows, gain_vector):
    values = full_rows.astype(jnp.float32)
    mean_square = jnp.mean(values * values, axis=-1, keepdims=True)
    return values * lax.rsqrt(mean_square + epsilon) * gain_vector


def shards(
    support_tokens,
    support_lengths,
    support_labels,
    query_tokens,
    query_lengths,
    query_episodes,
    embedding,
    attn_gain,
    query_weight,
    key_weight,
    value_weight,
    out_weight,
    final_gain,
):
    group_count = lax.axis_size(("dp", "pipe"))
    sections = lax.axis_size("pipe")
    sup_dev, seq_len = support_tokens.shape
    qry_dev = query_tokens.shape[0]
    seq_count = sup_dev + qry_dev
    row_count = seq_count * seq_len
    table_rows, width = embedding.shape
    column_start = lax.axis_index("tensor") * width
    all_support, all_query, every_sup_len, every_qry_len = (
        lax.all_gather(support_tokens, ("dp", "pipe"), axis=0, tiled=True),
        lax.all_gather(query_tokens, ("dp", "pipe"), axis=0, tiled=True),
        lax.all_gather(support_lengths, ("dp", "pipe"), axis=0, tiled=True),
        lax.all_gather(query_lengths, ("dp", "pipe"), axis=0, tiled=True),
    )
    token_flat = jnp.concatenate(
        [all_support.reshape(group_count, sup_dev * seq_len), all_query], axis=1
    ).reshape(group_count * row_count)
    local_ids = token_flat - lax.axis_index(("dp", "pipe")) * table_rows
    inside = (local_ids >= 0) & (local_ids < table_rows)
    picked = jnp.take(embedding, jnp.clip(local_ids, 0, table_rows - 1), axis=0)
    picked = jnp.where(inside[:, None], picked, jnp.zeros_like(picked))
    hidden = lax.psum_scatter(
        picked.astype(jnp.float32).astype(jnp.bfloat16),
        ("dp", "pipe"),
        scatter_dimension=0,
        tiled=True,
    )
    seq_lengths = jnp.concatenate([support_lengths, query_lengths], axis=0)
    query_proj = query_weight[0]
    key_proj = key_weight[0]
    value_proj = value_weight[0]
    out_proj = out_weight[0]
    gain_vector = attn_gain[0]
    local_heads = query_proj.shape[1] // HEAD_DIM
    local_groups = key_proj.shape[1] // HEAD_DIM
    group_size = local_heads // local_groups
    w_in = jnp.concatenate([query_proj, key_proj, value_proj], axis=1)
    query_cols = local_heads * HEAD_DIM
    key_cols = local_groups * HEAD_DIM
    positions = jnp.arange(seq_len)
    causal = positions[None, :] <= positions[:, None]

    def section_block(stream, lengths_here):
        normed = whole_values(whole_rows(stream), gain_vector).astype(jnp.bfloat16)
        projected = jnp.dot(normed, w_in, preferred_element_type=jnp.float32)
        query_heads = projected[:, :query_cols].reshape(seq_count, seq_len, local_heads, HEAD_DIM)
        key_heads = projected[:, query_cols : query_cols + key_cols].reshape(
            seq_count, seq_len, local_groups, HEAD_DIM
        )
        value_heads = (
            projected[:, query_cols + key_cols :]
            .reshape(seq_count, seq_len, local_groups, HEAD_DIM)
            .astype(jnp.bfloat16)
        )
        query_heads = (
            rotate(query_heads, seq_len)
            .astype(jnp.bfloat16)
            .reshape(seq_count, seq_len, local_groups, group_size, HEAD_DIM)
        )
        key_heads = rotate(key_heads, seq_len).astype(jnp.bfloat16)
        scores = jnp.einsum(
            "sikgd,sjkd->skgij", query_heads, key_heads, preferred_element_type=jnp.float32
        ) / math.sqrt(HEAD_DIM)
        visible = causal[None, :, :] & (positions[None, None, :] < lengths_here[:, None, None])
        scores = jnp.where(visible[:, None, None, :, :], scores, -1e30)
        weights = jax.nn.softmax(scores, axis=-1).astype(jnp.bfloat16)
        mixed = jnp.einsum(
            "skgij,sjkd->sikgd", weights, value_heads, preferred_element_type=jnp.float32
        )
        mixed = mixed.astype(jnp.bfloat16).reshape(row_count, query_cols)
        partial_out = jnp.dot(mixed, out_proj, preferred_element_type=jnp.float32)
        summed = lax.psum_scatter(
            partial_out.astype(jnp.bfloat16), "tensor", scatter_dimension=1, tiled=True
        ).astype(jnp.float32)
        return (stream.astype(jnp.float32) + summed).astype(jnp.bfloat16)

    section_index = lax.axis_index("pipe")
    dp_base = lax.axis_index("dp") * sections

    def tick(tick_index, stream):
        held_group = dp_base + (section_index - tick_index) % sections
        sup_part = lax.dynamic_slice_in_dim(every_sup_len, held_group * sup_dev, sup_dev)
        qry_part = lax.dynamic_slice_in_dim(every_qry_len, held_group * qry_dev, qry_dev)
        lengths_here = jnp.concatenate([sup_part, qry_part], axis=0)
        first_tick = (tick_index - section_index) % sections
        active = (first_tick <= tick_index) & (tick_index < first_tick + sections)
        computed = section_block(stream, lengths_here)
        stream = jnp.where(active, computed, stream)
        return passed_along(stream, "pipe", 1)

    hidden = lax.fori_loop(0, 2 * sections, tick, hidden)
    final = lax.dynamic_slice_in_dim(
        whole_values(whole_rows(hidden), final_gain), column_start, width, 1
    )
    live = (positions[None, :] < seq_lengths[:, None]).astype(jnp.float32)
    pooled = jnp.sum(
        final.reshape(seq_count, seq_len, width) * live[:, :, None], axis=1
    ) / seq_lengths[:, None].astype(jnp.float32)
    support_pooled = pooled[:sup_dev]
    query_pooled = pooled[sup_dev:]
    class_count_all = EPISODES * WAYS
    onehot = (support_labels[:, 0][:, None] == jnp.arange(class_count_all)[None, :]).astype(
        jnp.float32
    )
    class_total = jnp.dot(onehot.T, support_pooled, precision=lax.Precision.HIGHEST)
    class_count = jnp.sum(onehot, axis=0)
    class_total, class_count = (
        lax.psum(class_total.astype(jnp.bfloat16), ("dp", "pipe")).astype(jnp.float32),
        lax.psum(class_count.astype(jnp.bfloat16), ("dp", "pipe")).astype(jnp.float32),
    )
    prototypes = class_total / class_count[:, None]
    episode_pick = (query_episodes[:, None] == jnp.arange(EPISODES)[None, :]).astype(jnp.float32)
    chosen = jnp.einsum(
        "qe,ewc->qwc",
        episode_pick,
        prototypes.reshape(EPISODES, WAYS, width),
        precision=lax.Precision.HIGHEST,
    )
    partial_distance = jnp.sum((query_pooled[:, None, :] - chosen) ** 2, axis=-1)
    distance = lax.psum(partial_distance, "tensor")
    logits = -distance / math.sqrt(D)
    return (prototypes, logits)


def solution(mesh):
    return jax.shard_map(
        shards,
        mesh=mesh,
        in_specs=(
            P(("dp", "pipe"), None),
            P(("dp", "pipe")),
            P(("dp", "pipe"), None),
            P(("dp", "pipe"), None),
            P(("dp", "pipe")),
            P(("dp", "pipe")),
            P(("dp", "pipe"), "tensor"),
            P("pipe", None),
            P("pipe", None, "tensor"),
            P("pipe", None, "tensor"),
            P("pipe", None, "tensor"),
            P("pipe", "tensor", None),
            P(),
        ),
        out_specs=(P(None, "tensor"), P(("dp", "pipe"), None)),
        check_vma=False,
    )
```

profile of v0, /device:TPU:8, one launch (start us, length us, event | category | flops | bytes accessed | tf_op | source)
XLA Modules:
  0.0 830.7 jit_solution(18302538500788156600)
XLA Ops:
  7.2 29.0 %all-gather.1 = s32[16,1,32]{2,1,0:T(1,128)S(1)} all-gather(s32[1,1,32]{2,1,0:T(1,128)} %bitcast.117), channel_id=1, replica_groups=mesh['dp'=4,'pipe'=4,'tensor'=2] {'dp','pipe'}, dimensions={0}, use_global_device_ids=true | all-gather | bytes 2176 | tf_op jit(solution)/shard_map/all_gather | solution.py:72
  36.2 33.0 %all-gather = s32[16,2,32]{2,1,0:T(2,128)S(1)} all-gather(s32[1,2,32]{2,1,0:T(2,128)} %bitcast.113), channel_id=1, replica_groups=mesh['dp'=4,'pipe'=4,'tensor'=2] {'dp','pipe'}, dimensions={0}, use_global_device_ids=true | all-gather | bytes 4352 | tf_op jit(solution)/shard_map/all_gather | solution.py:71
  69.7 20.5 %gather_fusion = bf16[1536,2048]{1,0:T(8,128)(2,1)} fusion(bf16[4008,2048]{1,0:T(8,128)(2,1)} %param.21, s32[2048]{0:T(1024)S(1)} %pad_clamp_fusion), kind=kCustom, calls=%fused_computation | custom fusion | bytes 12589056 | tf_op jit(solution)/shard_map/jit(_take)/gather | solution.py:81
  108.2 18.7 %pad_maximum_fusion = bf16[4096,3072]{1,0:T(8,128)(2,1)} fusion(bf16[4096,512]{1,0:T(8,128)(2,1)} %bitcast.104, bf16[4096,512]{1,0:T(8,128)(2,1)} %bitcast.105, bf16[4096,2048]{1,0:T(8,128)(2,1)} %bitcast.99), kind=kLoop, calls=%fused_computation.54 | loop fusion | flops 75497472 | bytes 50331648 | tf_op jit(solution)/shard_map/concatenate | solution.py:98
  126.8 53.5 %reduce-scatter.3.cloned.1.call-done = bf16[96,2048]{1,0:T(8,128)(2,1)} async-done(((bf16[1536,2048]{1,0:T(8,128)(2,1)}), bf16[96,2048]{1,0:T(8,128)(2,1)}) %reduce-scatter.3.cloned.1.call-update) | async-done | bytes 393232 | tf_op jit(solution)/shard_map/reduce_scatter | solution.py:83
  180.3 532.5 %while.16 = (s32[]{:T(128)}, bf16[96,2048]{1,0:T(8,128)(2,1)}, s32[]{:T(128)}, f32[1,4096]{1,0:T(1,128)S(1)}, bf16[4096,3072]{1,0:T(8,128)(2,1)}, /*index=5*/s32...) while((s32[]{:T(128)}, bf16[96,2048]{1,0:T(8,128)(2,1)}, ...), condition=%wide.region_6.7_spmd.clone, body=%wide.region_1.0_spmd.clone.sunk | while | flops 4072005120 | bytes 66611072 | solution.py:152
  180.4 11.0 %all_gather.32 = bf16[96,4096]{1,0:T(8,128)(2,1)S(1)} all-gather(bf16[96,2048]{1,0:T(8,128)(2,1)} %get-tuple-element.408), channel_id=1, replica_groups=mesh['dp'=4,'pipe'=4,'tensor'=2] {'tensor'}, dimensions={1}, use_global_device_ids=true | all-gather | bytes 1179648 | tf_op jit(solution)/shard_map/while/body/eval_jaxpr/all_gather | solution.py:38
  191.6 10.4 %fusion.89 = f32[96,3072]{1,0:T(8,128)S(1)} fusion(bf16[4096,3072]{1,0:T(8,128)(2,1)} %get-tuple-element.427, bf16[96,4096]{1,0:T(8,128)(2,1)S(1)} %all_gather.32, f32[4096]{0:T(1024)S(1)} %bitcast.108, f32[96]{0:T(128)S(1)} %add_rsqrt_fusion.3), kind=kOutput, calls=%fused_computation.17.clone.1 | convolution fusion | flops 2417491968 | bytes 27148672 | tf_op jit(solution)/shard_map/while/body/eval_jaxpr/dot_general | solution.py:106
  207.3 9.5 %convolution_convert_fusion.4 = bf16[96,4096]{1,0:T(8,128)(2,1)} fusion(bf16[96,2048]{1,0:T(8,128)(2,1)S(1)} %reshape.325, bf16[2048,4096]{1,0:T(8,128)(2,1)} %get-tuple-element.431), kind=kOutput, calls=%fused_computation.4.clone.1 | convolution fusion | flops 1611005952 | bytes 17956864 | tf_op jit(solution)/shard_map/while/body/eval_jaxpr/dot_general | solution.py:132
  216.9 17.6 %reduce-scatter.5.cloned.1.call-done = bf16[96,2048]{1,0:T(8,128)(2,1)} async-done(((bf16[96,4096]{1,0:T(8,128)(2,1)}), bf16[96,2048]{1,0:T(8,128)(2,1)}) %reduce-scatter.5.cloned.1.call-update) | async-done | bytes 393232 | tf_op jit(solution)/shard_map/while/body/eval_jaxpr/reduce_scatter | solution.py:133
  237.1 9.2 %collective-permute-done = bf16[96,2048]{1,0:T(8,128)(2,1)S(1)} collective-permute-done((bf16[96,2048]{1,0:T(8,128)(2,1)S(1)}, bf16[96,2048]{1,0:T(8,128)(2,1)S(1)}, u32[]{:S(2)}, u32[]{:S(2)}) %collective-permute-start) | collective-permute-done | bytes 393248 | tf_op jit(solution)/shard_map/while/body/eval_jaxpr/ppermute | solution.py:18
  247.2 10.7 %all_gather.32 = bf16[96,4096]{1,0:T(8,128)(2,1)S(1)} all-gather(bf16[96,2048]{1,0:T(8,128)(2,1)} %get-tuple-element.408), channel_id=1, replica_groups=mesh['dp'=4,'pipe'=4,'tensor'=2] {'tensor'}, dimensions={1}, use_global_device_ids=true | all-gather | bytes 1179648 | tf_op jit(solution)/shard_map/while/body/eval_jaxpr/all_gather | solution.py:38
  258.1 10.4 %fusion.89 = f32[96,3072]{1,0:T(8,128)S(1)} fusion(bf16[4096,3072]{1,0:T(8,128)(2,1)} %get-tuple-element.427, bf16[96,4096]{1,0:T(8,128)(2,1)S(1)} %all_gather.32, f32[4096]{0:T(1024)S(1)} %bitcast.108, f32[96]{0:T(128)S(1)} %add_rsqrt_fusion.3), kind=kOutput, calls=%fused_computation.17.clone.1 | convolution fusion | flops 2417491968 | bytes 27148672 | tf_op jit(solution)/shard_map/while/body/eval_jaxpr/dot_general | solution.py:106
  273.8 9.5 %convolution_convert_fusion.4 = bf16[96,4096]{1,0:T(8,128)(2,1)} fusion(bf16[96,2048]{1,0:T(8,128)(2,1)S(1)} %reshape.325, bf16[2048,4096]{1,0:T(8,128)(2,1)} %get-tuple-element.431), kind=kOutput, calls=%fused_computation.4.clone.1 | convolution fusion | flops 1611005952 | bytes 17956864 | tf_op jit(solution)/shard_map/while/body/eval_jaxpr/dot_general | solution.py:132
  283.4 17.6 %reduce-scatter.5.cloned.1.call-done = bf16[96,2048]{1,0:T(8,128)(2,1)} async-done(((bf16[96,4096]{1,0:T(8,128)(2,1)}), bf16[96,2048]{1,0:T(8,128)(2,1)}) %reduce-scatter.5.cloned.1.call-update) | async-done | bytes 393232 | tf_op jit(solution)/shard_map/while/body/eval_jaxpr/reduce_scatter | solution.py:133
  303.7 9.2 %collective-permute-done = bf16[96,2048]{1,0:T(8,128)(2,1)S(1)} collective-permute-done((bf16[96,2048]{1,0:T(8,128)(2,1)S(1)}, bf16[96,2048]{1,0:T(8,128)(2,1)S(1)}, u32[]{:S(2)}, u32[]{:S(2)}) %collective-permute-start) | collective-permute-done | bytes 393248 | tf_op jit(solution)/shard_map/while/body/eval_jaxpr/ppermute | solution.py:18
  313.7 10.7 %all_gather.32 = bf16[96,4096]{1,0:T(8,128)(2,1)S(1)} all-gather(bf16[96,2048]{1,0:T(8,128)(2,1)} %get-tuple-element.408), channel_id=1, replica_groups=mesh['dp'=4,'pipe'=4,'tensor'=2] {'tensor'}, dimensions={1}, use_global_device_ids=true | all-gather | bytes 1179648 | tf_op jit(solution)/shard_map/while/body/eval_jaxpr/all_gather | solution.py:38
  324.6 10.4 %fusion.89 = f32[96,3072]{1,0:T(8,128)S(1)} fusion(bf16[4096,3072]{1,0:T(8,128)(2,1)} %get-tuple-element.427, bf16[96,4096]{1,0:T(8,128)(2,1)S(1)} %all_gather.32, f32[4096]{0:T(1024)S(1)} %bitcast.108, f32[96]{0:T(128)S(1)} %add_rsqrt_fusion.3), kind=kOutput, calls=%fused_computation.17.clone.1 | convolution fusion | flops 2417491968 | bytes 27148672 | tf_op jit(solution)/shard_map/while/body/eval_jaxpr/dot_general | solution.py:106
  340.3 9.5 %convolution_convert_fusion.4 = bf16[96,4096]{1,0:T(8,128)(2,1)} fusion(bf16[96,2048]{1,0:T(8,128)(2,1)S(1)} %reshape.325, bf16[2048,4096]{1,0:T(8,128)(2,1)} %get-tuple-element.431), kind=kOutput, calls=%fused_computation.4.clone.1 | convolution fusion | flops 1611005952 | bytes 17956864 | tf_op jit(solution)/shard_map/while/body/eval_jaxpr/dot_general | solution.py:132
  349.9 17.7 %reduce-scatter.5.cloned.1.call-done = bf16[96,2048]{1,0:T(8,128)(2,1)} async-done(((bf16[96,4096]{1,0:T(8,128)(2,1)}), bf16[96,2048]{1,0:T(8,128)(2,1)}) %reduce-scatter.5.cloned.1.call-update) | async-done | bytes 393232 | tf_op jit(solution)/shard_map/while/body/eval_jaxpr/reduce_scatter | solution.py:133
  380.2 10.7 %all_gather.32 = bf16[96,4096]{1,0:T(8,128)(2,1)S(1)} all-gather(bf16[96,2048]{1,0:T(8,128)(2,1)} %get-tuple-element.408), channel_id=1, replica_groups=mesh['dp'=4,'pipe'=4,'tensor'=2] {'tensor'}, dimensions={1}, use_global_device_ids=true | all-gather | bytes 1179648 | tf_op jit(solution)/shard_map/while/body/eval_jaxpr/all_gather | solution.py:38
  391.2 10.4 %fusion.89 = f32[96,3072]{1,0:T(8,128)S(1)} fusion(bf16[4096,3072]{1,0:T(8,128)(2,1)} %get-tuple-element.427, bf16[96,4096]{1,0:T(8,128)(2,1)S(1)} %all_gather.32, f32[4096]{0:T(1024)S(1)} %bitcast.108, f32[96]{0:T(128)S(1)} %add_rsqrt_fusion.3), kind=kOutput, calls=%fused_computation.17.clone.1 | convolution fusion | flops 2417491968 | bytes 27148672 | tf_op jit(solution)/shard_map/while/body/eval_jaxpr/dot_general | solution.py:106
  406.8 9.5 %convolution_convert_fusion.4 = bf16[96,4096]{1,0:T(8,128)(2,1)} fusion(bf16[96,2048]{1,0:T(8,128)(2,1)S(1)} %reshape.325, bf16[2048,4096]{1,0:T(8,128)(2,1)} %get-tuple-element.431), kind=kOutput, calls=%fused_computation.4.clone.1 | convolution fusion | flops 1611005952 | bytes 17956864 | tf_op jit(solution)/shard_map/while/body/eval_jaxpr/dot_general | solution.py:132
  416.4 17.6 %reduce-scatter.5.cloned.1.call-done = bf16[96,2048]{1,0:T(8,128)(2,1)} async-done(((bf16[96,4096]{1,0:T(8,128)(2,1)}), bf16[96,2048]{1,0:T(8,128)(2,1)}) %reduce-scatter.5.cloned.1.call-update) | async-done | bytes 393232 | tf_op jit(solution)/shard_map/while/body/eval_jaxpr/reduce_scatter | solution.py:133
  436.7 9.2 %collective-permute-done = bf16[96,2048]{1,0:T(8,128)(2,1)S(1)} collective-permute-done((bf16[96,2048]{1,0:T(8,128)(2,1)S(1)}, bf16[96,2048]{1,0:T(8,128)(2,1)S(1)}, u32[]{:S(2)}, u32[]{:S(2)}) %collective-permute-start) | collective-permute-done | bytes 393248 | tf_op jit(solution)/shard_map/while/body/eval_jaxpr/ppermute | solution.py:18
  446.7 10.7 %all_gather.32 = bf16[96,4096]{1,0:T(8,128)(2,1)S(1)} all-gather(bf16[96,2048]{1,0:T(8,128)(2,1)} %get-tuple-element.408), channel_id=1, replica_groups=mesh['dp'=4,'pipe'=4,'tensor'=2] {'tensor'}, dimensions={1}, use_global_device_ids=true | all-gather | bytes 1179648 | tf_op jit(solution)/shard_map/while/body/eval_jaxpr/all_gather | solution.py:38
  457.7 10.4 %fusion.89 = f32[96,3072]{1,0:T(8,128)S(1)} fusion(bf16[4096,3072]{1,0:T(8,128)(2,1)} %get-tuple-element.427, bf16[96,4096]{1,0:T(8,128)(2,1)S(1)} %all_gather.32, f32[4096]{0:T(1024)S(1)} %bitcast.108, f32[96]{0:T(128)S(1)} %add_rsqrt_fusion.3), kind=kOutput, calls=%fused_computation.17.clone.1 | convolution fusion | flops 2417491968 | bytes 27148672 | tf_op jit(solution)/shard_map/while/body/eval_jaxpr/dot_general | solution.py:106
  473.4 9.5 %convolution_convert_fusion.4 = bf16[96,4096]{1,0:T(8,128)(2,1)} fusion(bf16[96,2048]{1,0:T(8,128)(2,1)S(1)} %reshape.325, bf16[2048,4096]{1,0:T(8,128)(2,1)} %get-tuple-element.431), kind=kOutput, calls=%fused_computation.4.clone.1 | convolution fusion | flops 1611005952 | bytes 17956864 | tf_op jit(solution)/shard_map/while/body/eval_jaxpr/dot_general | solution.py:132
  483.0 17.6 %reduce-scatter.5.cloned.1.call-done = bf16[96,2048]{1,0:T(8,128)(2,1)} async-done(((bf16[96,4096]{1,0:T(8,128)(2,1)}), bf16[96,2048]{1,0:T(8,128)(2,1)}) %reduce-scatter.5.cloned.1.call-update) | async-done | bytes 393232 | tf_op jit(solution)/shard_map/while/body/eval_jaxpr/reduce_scatter | solution.py:133
  503.3 9.2 %collective-permute-done = bf16[96,2048]{1,0:T(8,128)(2,1)S(1)} collective-permute-done((bf16[96,2048]{1,0:T(8,128)(2,1)S(1)}, bf16[96,2048]{1,0:T(8,128)(2,1)S(1)}, u32[]{:S(2)}, u32[]{:S(2)}) %collective-permute-start) | collective-permute-done | bytes 393248 | tf_op jit(solution)/shard_map/while/body/eval_jaxpr/ppermute | solution.py:18
  513.3 10.7 %all_gather.32 = bf16[96,4096]{1,0:T(8,128)(2,1)S(1)} all-gather(bf16[96,2048]{1,0:T(8,128)(2,1)} %get-tuple-element.408), channel_id=1, replica_groups=mesh['dp'=4,'pipe'=4,'tensor'=2] {'tensor'}, dimensions={1}, use_global_device_ids=true | all-gather | bytes 1179648 | tf_op jit(solution)/shard_map/while/body/eval_jaxpr/all_gather | solution.py:38
  524.2 10.4 %fusion.89 = f32[96,3072]{1,0:T(8,128)S(1)} fusion(bf16[4096,3072]{1,0:T(8,128)(2,1)} %get-tuple-element.427, bf16[96,4096]{1,0:T(8,128)(2,1)S(1)} %all_gather.32, f32[4096]{0:T(1024)S(1)} %bitcast.108, f32[96]{0:T(128)S(1)} %add_rsqrt_fusion.3), kind=kOutput, calls=%fused_computation.17.clone.1 | convolution fusion | flops 2417491968 | bytes 27148672 | tf_op jit(solution)/shard_map/while/body/eval_jaxpr/dot_general | solution.py:106
  539.9 9.5 %convolution_convert_fusion.4 = bf16[96,4096]{1,0:T(8,128)(2,1)} fusion(bf16[96,2048]{1,0:T(8,128)(2,1)S(1)} %reshape.325, bf16[2048,4096]{1,0:T(8,128)(2,1)} %get-tuple-element.431), kind=kOutput, calls=%fused_computation.4.clone.1 | convolution fusion | flops 1611005952 | bytes 17956864 | tf_op jit(solution)/shard_map/while/body/eval_jaxpr/dot_general | solution.py:132
  549.5 17.6 %reduce-scatter.5.cloned.1.call-done = bf16[96,2048]{1,0:T(8,128)(2,1)} async-done(((bf16[96,4096]{1,0:T(8,128)(2,1)}), bf16[96,2048]{1,0:T(8,128)(2,1)}) %reduce-scatter.5.cloned.1.call-update) | async-done | bytes 393232 | tf_op jit(solution)/shard_map/while/body/eval_jaxpr/reduce_scatter | solution.py:133
  569.8 9.2 %collective-permute-done = bf16[96,2048]{1,0:T(8,128)(2,1)S(1)} collective-permute-done((bf16[96,2048]{1,0:T(8,128)(2,1)S(1)}, bf16[96,2048]{1,0:T(8,128)(2,1)S(1)}, u32[]{:S(2)}, u32[]{:S(2)}) %collective-permute-start) | collective-permute-done | bytes 393248 | tf_op jit(solution)/shard_map/while/body/eval_jaxpr/ppermute | solution.py:18
  579.8 10.7 %all_gather.32 = bf16[96,4096]{1,0:T(8,128)(2,1)S(1)} all-gather(bf16[96,2048]{1,0:T(8,128)(2,1)} %get-tuple-element.408), channel_id=1, replica_groups=mesh['dp'=4,'pipe'=4,'tensor'=2] {'tensor'}, dimensions={1}, use_global_device_ids=true | all-gather | bytes 1179648 | tf_op jit(solution)/shard_map/while/body/eval_jaxpr/all_gather | solution.py:38
  590.8 10.4 %fusion.89 = f32[96,3072]{1,0:T(8,128)S(1)} fusion(bf16[4096,3072]{1,0:T(8,128)(2,1)} %get-tuple-element.427, bf16[96,4096]{1,0:T(8,128)(2,1)S(1)} %all_gather.32, f32[4096]{0:T(1024)S(1)} %bitcast.108, f32[96]{0:T(128)S(1)} %add_rsqrt_fusion.3), kind=kOutput, calls=%fused_computation.17.clone.1 | convolution fusion | flops 2417491968 | bytes 27148672 | tf_op jit(solution)/shard_map/while/body/eval_jaxpr/dot_general | solution.py:106
  606.5 9.5 %convolution_convert_fusion.4 = bf16[96,4096]{1,0:T(8,128)(2,1)} fusion(bf16[96,2048]{1,0:T(8,128)(2,1)S(1)} %reshape.325, bf16[2048,4096]{1,0:T(8,128)(2,1)} %get-tuple-element.431), kind=kOutput, calls=%fused_computation.4.clone.1 | convolution fusion | flops 1611005952 | bytes 17956864 | tf_op jit(solution)/shard_map/while/body/eval_jaxpr/dot_general | solution.py:132
  616.0 17.6 %reduce-scatter.5.cloned.1.call-done = bf16[96,2048]{1,0:T(8,128)(2,1)} async-done(((bf16[96,4096]{1,0:T(8,128)(2,1)}), bf16[96,2048]{1,0:T(8,128)(2,1)}) %reduce-scatter.5.cloned.1.call-update) | async-done | bytes 393232 | tf_op jit(solution)/shard_map/while/body/eval_jaxpr/reduce_scatter | solution.py:133
  636.3 9.2 %collective-permute-done = bf16[96,2048]{1,0:T(8,128)(2,1)S(1)} collective-permute-done((bf16[96,2048]{1,0:T(8,128)(2,1)S(1)}, bf16[96,2048]{1,0:T(8,128)(2,1)S(1)}, u32[]{:S(2)}, u32[]{:S(2)}) %collective-permute-start) | collective-permute-done | bytes 393248 | tf_op jit(solution)/shard_map/while/body/eval_jaxpr/ppermute | solution.py:18
  646.3 10.7 %all_gather.32 = bf16[96,4096]{1,0:T(8,128)(2,1)S(1)} all-gather(bf16[96,2048]{1,0:T(8,128)(2,1)} %get-tuple-element.408), channel_id=1, replica_groups=mesh['dp'=4,'pipe'=4,'tensor'=2] {'tensor'}, dimensions={1}, use_global_device_ids=true | all-gather | bytes 1179648 | tf_op jit(solution)/shard_map/while/body/eval_jaxpr/all_gather | solution.py:38
  657.3 10.4 %fusion.89 = f32[96,3072]{1,0:T(8,128)S(1)} fusion(bf16[4096,3072]{1,0:T(8,128)(2,1)} %get-tuple-element.427, bf16[96,4096]{1,0:T(8,128)(2,1)S(1)} %all_gather.32, f32[4096]{0:T(1024)S(1)} %bitcast.108, f32[96]{0:T(128)S(1)} %add_rsqrt_fusion.3), kind=kOutput, calls=%fused_computation.17.clone.1 | convolution fusion | flops 2417491968 | bytes 27148672 | tf_op jit(solution)/shard_map/while/body/eval_jaxpr/dot_general | solution.py:106
  673.0 9.5 %convolution_convert_fusion.4 = bf16[96,4096]{1,0:T(8,128)(2,1)} fusion(bf16[96,2048]{1,0:T(8,128)(2,1)S(1)} %reshape.325, bf16[2048,4096]{1,0:T(8,128)(2,1)} %get-tuple-element.431), kind=kOutput, calls=%fused_computation.4.clone.1 | convolution fusion | flops 1611005952 | bytes 17956864 | tf_op jit(solution)/shard_map/while/body/eval_jaxpr/dot_general | solution.py:132
  682.5 17.6 %reduce-scatter.5.cloned.1.call-done = bf16[96,2048]{1,0:T(8,128)(2,1)} async-done(((bf16[96,4096]{1,0:T(8,128)(2,1)}), bf16[96,2048]{1,0:T(8,128)(2,1)}) %reduce-scatter.5.cloned.1.call-update) | async-done | bytes 393232 | tf_op jit(solution)/shard_map/while/body/eval_jaxpr/reduce_scatter | solution.py:133
  702.8 9.2 %collective-permute-done = bf16[96,2048]{1,0:T(8,128)(2,1)S(1)} collective-permute-done((bf16[96,2048]{1,0:T(8,128)(2,1)S(1)}, bf16[96,2048]{1,0:T(8,128)(2,1)S(1)}, u32[]{:S(2)}, u32[]{:S(2)}) %collective-permute-start) | collective-permute-done | bytes 393248 | tf_op jit(solution)/shard_map/while/body/eval_jaxpr/ppermute | solution.py:18
  712.8 10.8 %all_gather.29 = bf16[96,4096]{1,0:T(8,128)(2,1)S(1)} all-gather(bf16[96,2048]{1,0:T(8,128)(2,1)} %get-tuple-element.268), channel_id=1, replica_groups=mesh['dp'=4,'pipe'=4,'tensor'=2] {'tensor'}, dimensions={1}, use_global_device_ids=true | all-gather | bytes 1179648 | tf_op jit(solution)/shard_map/all_gather | solution.py:38
  725.6 32.3 %psum.22 = bf16[32]{0:T(256)(128)(2,1)S(1)} all-reduce(bf16[32]{0:T(256)(128)(2,1)S(1)} %convert_reduce_fusion), channel_id=1, replica_groups=mesh['dp'=4,'pipe'=4,'tensor'=2] {'dp','pipe'}, use_global_device_ids=true, to_apply=%region_11.12 | all-reduce | flops 32 | bytes 128 | tf_op jit(solution)/shard_map/psum | solution.py:170
  758.6 57.9 %all-reduce.5.cloned.1.call-done = bf16[32,2048]{1,0:T(8,128)(2,1)} async-done(((bf16[32,2048]{1,0:T(8,128)(2,1)}), bf16[32,2048]{1,0:T(8,128)(2,1)}) %all-reduce.5.cloned.1.call-update) | async-done | bytes 131088 | tf_op jit(solution)/shard_map/psum | solution.py:169
  (314 shorter events, 106.5 us)
Async XLA Ops:
  7.2 173.2 %reduce-scatter.3.cloned.1.call-start = ((), (), s32[]{:S(2)}) async-start(), calls=%async_computation.2 | async-start | bytes 6684672 | tf_op jit(solution)/shard_map/reduce_scatter | solution.py:83
  97.3 0.7 copy-start.6
  97.3 2.1 copy-start.5
  108.2 72.1 %copy-start.2 = (f32[1,4096]{1,0:T(1,128)S(1)}, f32[1,4096]{1,0:T(1,128)}, u32[]{:S(2)}) copy-start(f32[1,4096]{1,0:T(1,128)} %param.22) | copy-start | bytes 49156
  180.3 543.7 %dynamic-slice-start = ((f32[4096]{0:T(1024)}, s32[]{:T(128)}), f32[2048]{0:T(1024)S(1)}, s32[]{:S(2)}) async-start(f32[4096]{0:T(1024)} %param.27, s32[]{:T(128)} %select_n.115), calls=%async_computation.5 | async-start | bytes 16896 | tf_op jit(solution)/shard_map/dynamic_slice | solution.py:153
  180.3 54.2 %reduce-scatter.5.cloned.1.call-start = ((), (), s32[]{:S(2)}) async-start(), calls=%async_computation.4 | async-start | bytes 1179648 | tf_op jit(solution)/shard_map/while/body/eval_jaxpr/reduce_scatter | solution.py:133
  207.3 27.2 %copy-start = (bf16[96,2048]{1,0:T(8,128)(2,1)S(1)}, bf16[96,2048]{1,0:T(8,128)(2,1)}, u32[]{:S(2)}) copy-start(bf16[96,2048]{1,0:T(8,128)(2,1)} %get-tuple-element.408) | copy-start | bytes 1179652 | tf_op jit(solution)/shard_map/while
  235.6 10.8 %collective-permute-start = (bf16[96,2048]{1,0:T(8,128)(2,1)S(1)}, bf16[96,2048]{1,0:T(8,128)(2,1)S(1)}, u32[]{:S(2)}, u32[]{:S(2)}) collective-permute-start(bf16[96,2048]{1,0:T(8,128)(2,1)S(1)} %fusion.94), channel_id=1, source_target_pairs={{6,0},{0,2},{2,4},{4,6},{7,1},{1,3},{3,5},{5,7},{14,8},{8,10},{10,... | collective-permute-start | bytes 1179656 | tf_op jit(solution)/shard_map/while/body/eval_jaxpr/ppermute | solution.py:18
  246.4 0.8 copy-start.1
  247.1 53.9 %reduce-scatter.5.cloned.1.call-start = ((), (), s32[]{:S(2)}) async-start(), calls=%async_computation.4 | async-start | bytes 1179648 | tf_op jit(solution)/shard_map/while/body/eval_jaxpr/reduce_scatter | solution.py:133
  273.8 27.2 %copy-start = (bf16[96,2048]{1,0:T(8,128)(2,1)S(1)}, bf16[96,2048]{1,0:T(8,128)(2,1)}, u32[]{:S(2)}) copy-start(bf16[96,2048]{1,0:T(8,128)(2,1)} %get-tuple-element.408) | copy-start | bytes 1179652 | tf_op jit(solution)/shard_map/while
  302.1 10.7 %collective-permute-start = (bf16[96,2048]{1,0:T(8,128)(2,1)S(1)}, bf16[96,2048]{1,0:T(8,128)(2,1)S(1)}, u32[]{:S(2)}, u32[]{:S(2)}) collective-permute-start(bf16[96,2048]{1,0:T(8,128)(2,1)S(1)} %fusion.94), channel_id=1, source_target_pairs={{6,0},{0,2},{2,4},{4,6},{7,1},{1,3},{3,5},{5,7},{14,8},{8,10},{10,... | collective-permute-start | bytes 1179656 | tf_op jit(solution)/shard_map/while/body/eval_jaxpr/ppermute | solution.py:18
  312.9 0.8 copy-start.1
  313.6 53.9 %reduce-scatter.5.cloned.1.call-start = ((), (), s32[]{:S(2)}) async-start(), calls=%async_computation.4 | async-start | bytes 1179648 | tf_op jit(solution)/shard_map/while/body/eval_jaxpr/reduce_scatter | solution.py:133
  340.3 27.3 %copy-start = (bf16[96,2048]{1,0:T(8,128)(2,1)S(1)}, bf16[96,2048]{1,0:T(8,128)(2,1)}, u32[]{:S(2)}) copy-start(bf16[96,2048]{1,0:T(8,128)(2,1)} %get-tuple-element.408) | copy-start | bytes 1179652 | tf_op jit(solution)/shard_map/while
  368.7 10.7 %collective-permute-start = (bf16[96,2048]{1,0:T(8,128)(2,1)S(1)}, bf16[96,2048]{1,0:T(8,128)(2,1)S(1)}, u32[]{:S(2)}, u32[]{:S(2)}) collective-permute-start(bf16[96,2048]{1,0:T(8,128)(2,1)S(1)} %fusion.94), channel_id=1, source_target_pairs={{6,0},{0,2},{2,4},{4,6},{7,1},{1,3},{3,5},{5,7},{14,8},{8,10},{10,... | collective-permute-start | bytes 1179656 | tf_op jit(solution)/shard_map/while/body/eval_jaxpr/ppermute | solution.py:18
  379.4 0.8 copy-start.1
  380.2 53.9 %reduce-scatter.5.cloned.1.call-start = ((), (), s32[]{:S(2)}) async-start(), calls=%async_computation.4 | async-start | bytes 1179648 | tf_op jit(solution)/shard_map/while/body/eval_jaxpr/reduce_scatter | solution.py:133
  406.8 27.2 %copy-start = (bf16[96,2048]{1,0:T(8,128)(2,1)S(1)}, bf16[96,2048]{1,0:T(8,128)(2,1)}, u32[]{:S(2)}) copy-start(bf16[96,2048]{1,0:T(8,128)(2,1)} %get-tuple-element.408) | copy-start | bytes 1179652 | tf_op jit(solution)/shard_map/while
  435.2 10.8 %collective-permute-start = (bf16[96,2048]{1,0:T(8,128)(2,1)S(1)}, bf16[96,2048]{1,0:T(8,128)(2,1)S(1)}, u32[]{:S(2)}, u32[]{:S(2)}) collective-permute-start(bf16[96,2048]{1,0:T(8,128)(2,1)S(1)} %fusion.94), channel_id=1, source_target_pairs={{6,0},{0,2},{2,4},{4,6},{7,1},{1,3},{3,5},{5,7},{14,8},{8,10},{10,... | collective-permute-start | bytes 1179656 | tf_op jit(solution)/shard_map/while/body/eval_jaxpr/ppermute | solution.py:18
  445.9 0.8 copy-start.1
  446.7 53.9 %reduce-scatter.5.cloned.1.call-start = ((), (), s32[]{:S(2)}) async-start(), calls=%async_computation.4 | async-start | bytes 1179648 | tf_op jit(solution)/shard_map/while/body/eval_jaxpr/reduce_scatter | solution.py:133
  473.4 27.2 %copy-start = (bf16[96,2048]{1,0:T(8,128)(2,1)S(1)}, bf16[96,2048]{1,0:T(8,128)(2,1)}, u32[]{:S(2)}) copy-start(bf16[96,2048]{1,0:T(8,128)(2,1)} %get-tuple-element.408) | copy-start | bytes 1179652 | tf_op jit(solution)/shard_map/while
  501.7 10.7 %collective-permute-start = (bf16[96,2048]{1,0:T(8,128)(2,1)S(1)}, bf16[96,2048]{1,0:T(8,128)(2,1)S(1)}, u32[]{:S(2)}, u32[]{:S(2)}) collective-permute-start(bf16[96,2048]{1,0:T(8,128)(2,1)S(1)} %fusion.94), channel_id=1, source_target_pairs={{6,0},{0,2},{2,4},{4,6},{7,1},{1,3},{3,5},{5,7},{14,8},{8,10},{10,... | collective-permute-start | bytes 1179656 | tf_op jit(solution)/shard_map/while/body/eval_jaxpr/ppermute | solution.py:18
  512.5 0.8 copy-start.1
  513.2 53.9 %reduce-scatter.5.cloned.1.call-start = ((), (), s32[]{:S(2)}) async-start(), calls=%async_computation.4 | async-start | bytes 1179648 | tf_op jit(solution)/shard_map/while/body/eval_jaxpr/reduce_scatter | solution.py:133
  539.9 27.2 %copy-start = (bf16[96,2048]{1,0:T(8,128)(2,1)S(1)}, bf16[96,2048]{1,0:T(8,128)(2,1)}, u32[]{:S(2)}) copy-start(bf16[96,2048]{1,0:T(8,128)(2,1)} %get-tuple-element.408) | copy-start | bytes 1179652 | tf_op jit(solution)/shard_map/while
  568.2 10.8 %collective-permute-start = (bf16[96,2048]{1,0:T(8,128)(2,1)S(1)}, bf16[96,2048]{1,0:T(8,128)(2,1)S(1)}, u32[]{:S(2)}, u32[]{:S(2)}) collective-permute-start(bf16[96,2048]{1,0:T(8,128)(2,1)S(1)} %fusion.94), channel_id=1, source_target_pairs={{6,0},{0,2},{2,4},{4,6},{7,1},{1,3},{3,5},{5,7},{14,8},{8,10},{10,... | collective-permute-start | bytes 1179656 | tf_op jit(solution)/shard_map/while/body/eval_jaxpr/ppermute | solution.py:18
  579.0 0.8 copy-start.1
  579.8 53.8 %reduce-scatter.5.cloned.1.call-start = ((), (), s32[]{:S(2)}) async-start(), calls=%async_computation.4 | async-start | bytes 1179648 | tf_op jit(solution)/shard_map/while/body/eval_jaxpr/reduce_scatter | solution.py:133
  606.5 27.2 %copy-start = (bf16[96,2048]{1,0:T(8,128)(2,1)S(1)}, bf16[96,2048]{1,0:T(8,128)(2,1)}, u32[]{:S(2)}) copy-start(bf16[96,2048]{1,0:T(8,128)(2,1)} %get-tuple-element.408) | copy-start | bytes 1179652 | tf_op jit(solution)/shard_map/while
  634.8 10.8 %collective-permute-start = (bf16[96,2048]{1,0:T(8,128)(2,1)S(1)}, bf16[96,2048]{1,0:T(8,128)(2,1)S(1)}, u32[]{:S(2)}, u32[]{:S(2)}) collective-permute-start(bf16[96,2048]{1,0:T(8,128)(2,1)S(1)} %fusion.94), channel_id=1, source_target_pairs={{6,0},{0,2},{2,4},{4,6},{7,1},{1,3},{3,5},{5,7},{14,8},{8,10},{10,... | collective-permute-start | bytes 1179656 | tf_op jit(solution)/shard_map/while/body/eval_jaxpr/ppermute | solution.py:18
  645.5 0.8 copy-start.1
  646.3 53.9 %reduce-scatter.5.cloned.1.call-start = ((), (), s32[]{:S(2)}) async-start(), calls=%async_computation.4 | async-start | bytes 1179648 | tf_op jit(solution)/shard_map/while/body/eval_jaxpr/reduce_scatter | solution.py:133
  673.0 27.2 %copy-start = (bf16[96,2048]{1,0:T(8,128)(2,1)S(1)}, bf16[96,2048]{1,0:T(8,128)(2,1)}, u32[]{:S(2)}) copy-start(bf16[96,2048]{1,0:T(8,128)(2,1)} %get-tuple-element.408) | copy-start | bytes 1179652 | tf_op jit(solution)/shard_map/while
  701.3 10.7 %collective-permute-start = (bf16[96,2048]{1,0:T(8,128)(2,1)S(1)}, bf16[96,2048]{1,0:T(8,128)(2,1)S(1)}, u32[]{:S(2)}, u32[]{:S(2)}) collective-permute-start(bf16[96,2048]{1,0:T(8,128)(2,1)S(1)} %fusion.94), channel_id=1, source_target_pairs={{6,0},{0,2},{2,4},{4,6},{7,1},{1,3},{3,5},{5,7},{14,8},{8,10},{10,... | collective-permute-start | bytes 1179656 | tf_op jit(solution)/shard_map/while/body/eval_jaxpr/ppermute | solution.py:18
  712.0 0.8 copy-start.1
  712.8 11.6 %copy-start.4 = (s32[2,1]{0,1:T(1,128)S(1)}, s32[2,1]{0,1:T(1,128)}, u32[]{:S(2)}) copy-start(s32[2,1]{0,1:T(1,128)} %param.17) | copy-start | bytes 28
  712.8 103.8 %all-reduce.5.cloned.1.call-start = ((), (), s32[]{:S(2)}) async-start(), calls=%async_computation.3 | async-start | bytes 262144 | tf_op jit(solution)/shard_map/psum | solution.py:169
  817.6 6.3 copy-start.3
Sparse Core Ops, SparseCore 0:
  97.4 82.8 reduce-scatter.2
  217.0 17.4 reduce-scatter.4
  283.5 17.4 reduce-scatter.4
  350.0 17.5 reduce-scatter.4
  416.5 17.4 reduce-scatter.4
  483.1 17.5 reduce-scatter.4
  549.6 17.4 reduce-scatter.4
  616.1 17.4 reduce-scatter.4
  682.6 17.4 reduce-scatter.4
  725.7 90.8 all-reduce.4
where the time goes:
time: 832 us; the launch traced here: 831 us
  waiting for transfers between devices  326 us (39%)
  blocking collectives  204 us (25%)
  matrix products  177 us (21%)
  other arithmetic  50.2 us (6%)
  local copies, waits for them, and re-layouts  43.8 us (5%)
  between operations  16.2 us (2%)
  starting transfers between devices  12.4 us (1%)
    reduce_scatter x8, waiting for transfers between devices, section_block(): lax.psum_scatter(partial_out.astype(jnp.bfloat16), 'tensor', scatter_dime...  141 us
    all_gather x9, blocking collectives, whole_rows(): return lax.all_gather(hidden, 'tensor', axis=1, tiled=True)  96.8 us
    dot_general x8, matrix products, section_block(): projected = jnp.dot(normed, w_in, preferred_element_type=jnp.float32)  83.3 us
    dot_general x8, matrix products, section_block(): partial_out = jnp.dot(mixed, out_proj, preferred_element_type=jnp.float32)  76.2 us
    ppermute x8, waiting for transfers between devices, passed_along(): return lax.ppermute(block, axis, route)  73.6 us
    psum x1, waiting for transfers between devices, shards(): lax.psum(class_total.astype(jnp.bfloat16), ('dp', 'pipe'))  57.9 us
    reduce_scatter x1, waiting for transfers between devices, shards(): lax.psum_scatter(picked.astype(jnp.float32).astype(jnp.bfloat16), ('dp',...  53.5 us
    all_gather x1, blocking collectives, shards(): lax.all_gather(support_tokens, ('dp', 'pipe'), axis=0, tiled=True)  33 us
  transfers between devices with their start and end apart: 18, of which 18 were waited for; matrix products, arithmetic and copies ran while one was open for 2% of the time, Pallas kernels for 0%

commit v1 on v0

--- a/solution.py
+++ b/solution.py
@@ -165,8 +165,9 @@
     )
     class_total = jnp.dot(onehot.T, support_pooled, precision=lax.Precision.HIGHEST)
     class_count = jnp.sum(onehot, axis=0)
+    rest_patches = lambda x0: lax.all_gather(x0, ("dp", "pipe")).sum(axis=0)
     class_total, class_count = (
-        lax.psum(class_total.astype(jnp.bfloat16), ("dp", "pipe")).astype(jnp.float32),
+        rest_patches(class_total.astype(jnp.bfloat16)).astype(jnp.float32),
         lax.psum(class_count.astype(jnp.bfloat16), ("dp", "pipe")).astype(jnp.float32),
     )
     prototypes = class_total / class_count[:, None]

time: 832 us -> 785 us (0.944)
  waiting for transfers between devices: 326 us -> 276 us
    psum x1 -> x0, waiting for transfers between devices: 57.9 us -> none  [shards(): lax.psum(class_total.astype(jnp.bfloat16), ('dp', 'pipe'))]
  transfers between devices with their start and end apart: 18 -> 18, of which waited for: 18 -> 18; matrix products, arithmetic and copies ran while one was open for 2% -> 3% of each run, Pallas kernels for 0% -> 0%
where the time goes in v1:
time: 785 us; the launch traced here: 781 us
  waiting for transfers between devices  276 us (35%)
  blocking collectives  204 us (26%)
  matrix products  177 us (23%)
  other arithmetic  51.3 us (7%)
  local copies, waits for them, and re-layouts  43.8 us (6%)
  between operations  16.2 us (2%)
  starting transfers between devices  12.4 us (2%)
    reduce_scatter x8, waiting for transfers between devices, section_block(): lax.psum_scatter(partial_out.astype(jnp.bfloat16), 'tensor', scatter_dime...  141 us
    all_gather x9, blocking collectives, whole_rows(): return lax.all_gather(hidden, 'tensor', axis=1, tiled=True)  96.8 us
    dot_general x8, matrix products, section_block(): projected = jnp.dot(normed, w_in, preferred_element_type=jnp.float32)  83.3 us
    dot_general x8, matrix products, section_block(): partial_out = jnp.dot(mixed, out_proj, preferred_element_type=jnp.float32)  76.2 us
    ppermute x8, waiting for transfers between devices, passed_along(): return lax.ppermute(block, axis, route)  73.6 us
    reduce_scatter x1, waiting for transfers between devices, shards(): lax.psum_scatter(picked.astype(jnp.float32).astype(jnp.bfloat16), ('dp',...  53.5 us
    all_gather x1, blocking collectives, shards(): lax.all_gather(support_tokens, ('dp', 'pipe'), axis=0, tiled=True)  33 us
    psum x1, blocking collectives, shards(): lax.psum(class_count.astype(jnp.bfloat16), ('dp', 'pipe'))  32.5 us
  transfers between devices with their start and end apart: 18, of which 18 were waited for; matrix products, arithmetic and copies ran while one was open for 3% of the time, Pallas kernels for 0%

profile of v1, /device:TPU:8, one launch (start us, length us, event | category | flops | bytes accessed | tf_op | source)
XLA Modules:
  0.0 781.3 jit_solution(18366740458328289629)
XLA Ops:
  7.2 29.0 %all-gather.2 = s32[16,1,32]{2,1,0:T(1,128)S(1)} all-gather(s32[1,1,32]{2,1,0:T(1,128)} %bitcast.119), channel_id=1, replica_groups=mesh['dp'=4,'pipe'=4,'tensor'=2] {'dp','pipe'}, dimensions={0}, use_global_device_ids=true | all-gather | bytes 2176 | tf_op jit(solution)/shard_map/all_gather | solution.py:72
  36.2 33.0 %all-gather.1 = s32[16,2,32]{2,1,0:T(2,128)S(1)} all-gather(s32[1,2,32]{2,1,0:T(2,128)} %bitcast.115), channel_id=1, replica_groups=mesh['dp'=4,'pipe'=4,'tensor'=2] {'dp','pipe'}, dimensions={0}, use_global_device_ids=true | all-gather | bytes 4352 | tf_op jit(solution)/shard_map/all_gather | solution.py:71
  69.7 20.5 %gather_fusion = bf16[1536,2048]{1,0:T(8,128)(2,1)} fusion(bf16[4008,2048]{1,0:T(8,128)(2,1)} %param.21, s32[2048]{0:T(1024)S(1)} %pad_clamp_fusion), kind=kCustom, calls=%fused_computation | custom fusion | bytes 12589056 | tf_op jit(solution)/shard_map/jit(_take)/gather | solution.py:81
  108.2 18.7 %pad_maximum_fusion = bf16[4096,3072]{1,0:T(8,128)(2,1)} fusion(bf16[4096,512]{1,0:T(8,128)(2,1)} %bitcast.105, bf16[4096,512]{1,0:T(8,128)(2,1)} %bitcast.106, bf16[4096,2048]{1,0:T(8,128)(2,1)} %bitcast.100), kind=kLoop, calls=%fused_computation.54 | loop fusion | flops 75497472 | bytes 50331648 | tf_op jit(solution)/shard_map/concatenate | solution.py:98
  126.8 53.5 %reduce-scatter.3.cloned.1.call-done = bf16[96,2048]{1,0:T(8,128)(2,1)} async-done(((bf16[1536,2048]{1,0:T(8,128)(2,1)}), bf16[96,2048]{1,0:T(8,128)(2,1)}) %reduce-scatter.3.cloned.1.call-update) | async-done | bytes 393232 | tf_op jit(solution)/shard_map/reduce_scatter | solution.py:83
  180.3 532.5 %while.16 = (s32[]{:T(128)}, bf16[96,2048]{1,0:T(8,128)(2,1)}, s32[]{:T(128)}, f32[1,4096]{1,0:T(1,128)S(1)}, bf16[4096,3072]{1,0:T(8,128)(2,1)}, /*index=5*/s32...) while((s32[]{:T(128)}, bf16[96,2048]{1,0:T(8,128)(2,1)}, ...), condition=%wide.region_6.7_spmd.clone, body=%wide.region_1.0_spmd.clone.sunk | while | flops 4072005120 | bytes 66611072 | solution.py:152
  180.4 11.0 %all_gather.40 = bf16[96,4096]{1,0:T(8,128)(2,1)S(1)} all-gather(bf16[96,2048]{1,0:T(8,128)(2,1)} %get-tuple-element.408), channel_id=1, replica_groups=mesh['dp'=4,'pipe'=4,'tensor'=2] {'tensor'}, dimensions={1}, use_global_device_ids=true | all-gather | bytes 1179648 | tf_op jit(solution)/shard_map/while/body/eval_jaxpr/all_gather | solution.py:38
  191.6 10.4 %fusion.89 = f32[96,3072]{1,0:T(8,128)S(1)} fusion(bf16[4096,3072]{1,0:T(8,128)(2,1)} %get-tuple-element.427, bf16[96,4096]{1,0:T(8,128)(2,1)S(1)} %all_gather.40, f32[4096]{0:T(1024)S(1)} %bitcast.110, f32[96]{0:T(128)S(1)} %add_rsqrt_fusion.3), kind=kOutput, calls=%fused_computation.17.clone.1 | convolution fusion | flops 2417491968 | bytes 27148672 | tf_op jit(solution)/shard_map/while/body/eval_jaxpr/dot_general | solution.py:106
  207.3 9.5 %convolution_convert_fusion.4 = bf16[96,4096]{1,0:T(8,128)(2,1)} fusion(bf16[96,2048]{1,0:T(8,128)(2,1)S(1)} %reshape.355, bf16[2048,4096]{1,0:T(8,128)(2,1)} %get-tuple-element.431), kind=kOutput, calls=%fused_computation.4.clone.1 | convolution fusion | flops 1611005952 | bytes 17956864 | tf_op jit(solution)/shard_map/while/body/eval_jaxpr/dot_general | solution.py:132
  216.9 17.6 %reduce-scatter.5.cloned.1.call-done = bf16[96,2048]{1,0:T(8,128)(2,1)} async-done(((bf16[96,4096]{1,0:T(8,128)(2,1)}), bf16[96,2048]{1,0:T(8,128)(2,1)}) %reduce-scatter.5.cloned.1.call-update) | async-done | bytes 393232 | tf_op jit(solution)/shard_map/while/body/eval_jaxpr/reduce_scatter | solution.py:133
  237.1 9.2 %collective-permute-done = bf16[96,2048]{1,0:T(8,128)(2,1)S(1)} collective-permute-done((bf16[96,2048]{1,0:T(8,128)(2,1)S(1)}, bf16[96,2048]{1,0:T(8,128)(2,1)S(1)}, u32[]{:S(2)}, u32[]{:S(2)}) %collective-permute-start) | collective-permute-done | bytes 393248 | tf_op jit(solution)/shard_map/while/body/eval_jaxpr/ppermute | solution.py:18
  247.2 10.7 %all_gather.40 = bf16[96,4096]{1,0:T(8,128)(2,1)S(1)} all-gather(bf16[96,2048]{1,0:T(8,128)(2,1)} %get-tuple-element.408), channel_id=1, replica_groups=mesh['dp'=4,'pipe'=4,'tensor'=2] {'tensor'}, dimensions={1}, use_global_device_ids=true | all-gather | bytes 1179648 | tf_op jit(solution)/shard_map/while/body/eval_jaxpr/all_gather | solution.py:38
  258.1 10.4 %fusion.89 = f32[96,3072]{1,0:T(8,128)S(1)} fusion(bf16[4096,3072]{1,0:T(8,128)(2,1)} %get-tuple-element.427, bf16[96,4096]{1,0:T(8,128)(2,1)S(1)} %all_gather.40, f32[4096]{0:T(1024)S(1)} %bitcast.110, f32[96]{0:T(128)S(1)} %add_rsqrt_fusion.3), kind=kOutput, calls=%fused_computation.17.clone.1 | convolution fusion | flops 2417491968 | bytes 27148672 | tf_op jit(solution)/shard_map/while/body/eval_jaxpr/dot_general | solution.py:106
  273.8 9.5 %convolution_convert_fusion.4 = bf16[96,4096]{1,0:T(8,128)(2,1)} fusion(bf16[96,2048]{1,0:T(8,128)(2,1)S(1)} %reshape.355, bf16[2048,4096]{1,0:T(8,128)(2,1)} %get-tuple-element.431), kind=kOutput, calls=%fused_computation.4.clone.1 | convolution fusion | flops 1611005952 | bytes 17956864 | tf_op jit(solution)/shard_map/while/body/eval_jaxpr/dot_general | solution.py:132
  283.4 17.6 %reduce-scatter.5.cloned.1.call-done = bf16[96,2048]{1,0:T(8,128)(2,1)} async-done(((bf16[96,4096]{1,0:T(8,128)(2,1)}), bf16[96,2048]{1,0:T(8,128)(2,1)}) %reduce-scatter.5.cloned.1.call-update) | async-done | bytes 393232 | tf_op jit(solution)/shard_map/while/body/eval_jaxpr/reduce_scatter | solution.py:133
  303.7 9.2 %collective-permute-done = bf16[96,2048]{1,0:T(8,128)(2,1)S(1)} collective-permute-done((bf16[96,2048]{1,0:T(8,128)(2,1)S(1)}, bf16[96,2048]{1,0:T(8,128)(2,1)S(1)}, u32[]{:S(2)}, u32[]{:S(2)}) %collective-permute-start) | collective-permute-done | bytes 393248 | tf_op jit(solution)/shard_map/while/body/eval_jaxpr/ppermute | solution.py:18
  313.7 10.7 %all_gather.40 = bf16[96,4096]{1,0:T(8,128)(2,1)S(1)} all-gather(bf16[96,2048]{1,0:T(8,128)(2,1)} %get-tuple-element.408), channel_id=1, replica_groups=mesh['dp'=4,'pipe'=4,'tensor'=2] {'tensor'}, dimensions={1}, use_global_device_ids=true | all-gather | bytes 1179648 | tf_op jit(solution)/shard_map/while/body/eval_jaxpr/all_gather | solution.py:38
  324.6 10.4 %fusion.89 = f32[96,3072]{1,0:T(8,128)S(1)} fusion(bf16[4096,3072]{1,0:T(8,128)(2,1)} %get-tuple-element.427, bf16[96,4096]{1,0:T(8,128)(2,1)S(1)} %all_gather.40, f32[4096]{0:T(1024)S(1)} %bitcast.110, f32[96]{0:T(128)S(1)} %add_rsqrt_fusion.3), kind=kOutput, calls=%fused_computation.17.clone.1 | convolution fusion | flops 2417491968 | bytes 27148672 | tf_op jit(solution)/shard_map/while/body/eval_jaxpr/dot_general | solution.py:106
  340.3 9.5 %convolution_convert_fusion.4 = bf16[96,4096]{1,0:T(8,128)(2,1)} fusion(bf16[96,2048]{1,0:T(8,128)(2,1)S(1)} %reshape.355, bf16[2048,4096]{1,0:T(8,128)(2,1)} %get-tuple-element.431), kind=kOutput, calls=%fused_computation.4.clone.1 | convolution fusion | flops 1611005952 | bytes 17956864 | tf_op jit(solution)/shard_map/while/body/eval_jaxpr/dot_general | solution.py:132
  349.9 17.7 %reduce-scatter.5.cloned.1.call-done = bf16[96,2048]{1,0:T(8,128)(2,1)} async-done(((bf16[96,4096]{1,0:T(8,128)(2,1)}), bf16[96,2048]{1,0:T(8,128)(2,1)}) %reduce-scatter.5.cloned.1.call-update) | async-done | bytes 393232 | tf_op jit(solution)/shard_map/while/body/eval_jaxpr/reduce_scatter | solution.py:133
  370.2 9.2 %collective-permute-done = bf16[96,2048]{1,0:T(8,128)(2,1)S(1)} collective-permute-done((bf16[96,2048]{1,0:T(8,128)(2,1)S(1)}, bf16[96,2048]{1,0:T(8,128)(2,1)S(1)}, u32[]{:S(2)}, u32[]{:S(2)}) %collective-permute-start) | collective-permute-done | bytes 393248 | tf_op jit(solution)/shard_map/while/body/eval_jaxpr/ppermute | solution.py:18
  380.2 10.7 %all_gather.40 = bf16[96,4096]{1,0:T(8,128)(2,1)S(1)} all-gather(bf16[96,2048]{1,0:T(8,128)(2,1)} %get-tuple-element.408), channel_id=1, replica_groups=mesh['dp'=4,'pipe'=4,'tensor'=2] {'tensor'}, dimensions={1}, use_global_device_ids=true | all-gather | bytes 1179648 | tf_op jit(solution)/shard_map/while/body/eval_jaxpr/all_gather | solution.py:38
  391.2 10.4 %fusion.89 = f32[96,3072]{1,0:T(8,128)S(1)} fusion(bf16[4096,3072]{1,0:T(8,128)(2,1)} %get-tuple-element.427, bf16[96,4096]{1,0:T(8,128)(2,1)S(1)} %all_gather.40, f32[4096]{0:T(1024)S(1)} %bitcast.110, f32[96]{0:T(128)S(1)} %add_rsqrt_fusion.3), kind=kOutput, calls=%fused_computation.17.clone.1 | convolution fusion | flops 2417491968 | bytes 27148672 | tf_op jit(solution)/shard_map/while/body/eval_jaxpr/dot_general | solution.py:106
  406.8 9.5 %convolution_convert_fusion.4 = bf16[96,4096]{1,0:T(8,128)(2,1)} fusion(bf16[96,2048]{1,0:T(8,128)(2,1)S(1)} %reshape.355, bf16[2048,4096]{1,0:T(8,128)(2,1)} %get-tuple-element.431), kind=kOutput, calls=%fused_computation.4.clone.1 | convolution fusion | flops 1611005952 | bytes 17956864 | tf_op jit(solution)/shard_map/while/body/eval_jaxpr/dot_general | solution.py:132
  416.4 17.6 %reduce-scatter.5.cloned.1.call-done = bf16[96,2048]{1,0:T(8,128)(2,1)} async-done(((bf16[96,4096]{1,0:T(8,128)(2,1)}), bf16[96,2048]{1,0:T(8,128)(2,1)}) %reduce-scatter.5.cloned.1.call-update) | async-done | bytes 393232 | tf_op jit(solution)/shard_map/while/body/eval_jaxpr/reduce_scatter | solution.py:133
  436.7 9.2 %collective-permute-done = bf16[96,2048]{1,0:T(8,128)(2,1)S(1)} collective-permute-done((bf16[96,2048]{1,0:T(8,128)(2,1)S(1)}, bf16[96,2048]{1,0:T(8,128)(2,1)S(1)}, u32[]{:S(2)}, u32[]{:S(2)}) %collective-permute-start) | collective-permute-done | bytes 393248 | tf_op jit(solution)/shard_map/while/body/eval_jaxpr/ppermute | solution.py:18
  446.7 10.7 %all_gather.40 = bf16[96,4096]{1,0:T(8,128)(2,1)S(1)} all-gather(bf16[96,2048]{1,0:T(8,128)(2,1)} %get-tuple-element.408), channel_id=1, replica_groups=mesh['dp'=4,'pipe'=4,'tensor'=2] {'tensor'}, dimensions={1}, use_global_device_ids=true | all-gather | bytes 1179648 | tf_op jit(solution)/shard_map/while/body/eval_jaxpr/all_gather | solution.py:38
  457.7 10.4 %fusion.89 = f32[96,3072]{1,0:T(8,128)S(1)} fusion(bf16[4096,3072]{1,0:T(8,128)(2,1)} %get-tuple-element.427, bf16[96,4096]{1,0:T(8,128)(2,1)S(1)} %all_gather.40, f32[4096]{0:T(1024)S(1)} %bitcast.110, f32[96]{0:T(128)S(1)} %add_rsqrt_fusion.3), kind=kOutput, calls=%fused_computation.17.clone.1 | convolution fusion | flops 2417491968 | bytes 27148672 | tf_op jit(solution)/shard_map/while/body/eval_jaxpr/dot_general | solution.py:106
  473.4 9.5 %convolution_convert_fusion.4 = bf16[96,4096]{1,0:T(8,128)(2,1)} fusion(bf16[96,2048]{1,0:T(8,128)(2,1)S(1)} %reshape.355, bf16[2048,4096]{1,0:T(8,128)(2,1)} %get-tuple-element.431), kind=kOutput, calls=%fused_computation.4.clone.1 | convolution fusion | flops 1611005952 | bytes 17956864 | tf_op jit(solution)/shard_map/while/body/eval_jaxpr/dot_general | solution.py:132
  483.0 17.6 %reduce-scatter.5.cloned.1.call-done = bf16[96,2048]{1,0:T(8,128)(2,1)} async-done(((bf16[96,4096]{1,0:T(8,128)(2,1)}), bf16[96,2048]{1,0:T(8,128)(2,1)}) %reduce-scatter.5.cloned.1.call-update) | async-done | bytes 393232 | tf_op jit(solution)/shard_map/while/body/eval_jaxpr/reduce_scatter | solution.py:133
  503.3 9.2 %collective-permute-done = bf16[96,2048]{1,0:T(8,128)(2,1)S(1)} collective-permute-done((bf16[96,2048]{1,0:T(8,128)(2,1)S(1)}, bf16[96,2048]{1,0:T(8,128)(2,1)S(1)}, u32[]{:S(2)}, u32[]{:S(2)}) %collective-permute-start) | collective-permute-done | bytes 393248 | tf_op jit(solution)/shard_map/while/body/eval_jaxpr/ppermute | solution.py:18
  513.3 10.7 %all_gather.40 = bf16[96,4096]{1,0:T(8,128)(2,1)S(1)} all-gather(bf16[96,2048]{1,0:T(8,128)(2,1)} %get-tuple-element.408), channel_id=1, replica_groups=mesh['dp'=4,'pipe'=4,'tensor'=2] {'tensor'}, dimensions={1}, use_global_device_ids=true | all-gather | bytes 1179648 | tf_op jit(solution)/shard_map/while/body/eval_jaxpr/all_gather | solution.py:38
  524.2 10.4 %fusion.89 = f32[96,3072]{1,0:T(8,128)S(1)} fusion(bf16[4096,3072]{1,0:T(8,128)(2,1)} %get-tuple-element.427, bf16[96,4096]{1,0:T(8,128)(2,1)S(1)} %all_gather.40, f32[4096]{0:T(1024)S(1)} %bitcast.110, f32[96]{0:T(128)S(1)} %add_rsqrt_fusion.3), kind=kOutput, calls=%fused_computation.17.clone.1 | convolution fusion | flops 2417491968 | bytes 27148672 | tf_op jit(solution)/shard_map/while/body/eval_jaxpr/dot_general | solution.py:106
  539.9 9.5 %convolution_convert_fusion.4 = bf16[96,4096]{1,0:T(8,128)(2,1)} fusion(bf16[96,2048]{1,0:T(8,128)(2,1)S(1)} %reshape.355, bf16[2048,4096]{1,0:T(8,128)(2,1)} %get-tuple-element.431), kind=kOutput, calls=%fused_computation.4.clone.1 | convolution fusion | flops 1611005952 | bytes 17956864 | tf_op jit(solution)/shard_map/while/body/eval_jaxpr/dot_general | solution.py:132
  549.5 17.6 %reduce-scatter.5.cloned.1.call-done = bf16[96,2048]{1,0:T(8,128)(2,1)} async-done(((bf16[96,4096]{1,0:T(8,128)(2,1)}), bf16[96,2048]{1,0:T(8,128)(2,1)}) %reduce-scatter.5.cloned.1.call-update) | async-done | bytes 393232 | tf_op jit(solution)/shard_map/while/body/eval_jaxpr/reduce_scatter | solution.py:133
  569.8 9.2 %collective-permute-done = bf16[96,2048]{1,0:T(8,128)(2,1)S(1)} collective-permute-done((bf16[96,2048]{1,0:T(8,128)(2,1)S(1)}, bf16[96,2048]{1,0:T(8,128)(2,1)S(1)}, u32[]{:S(2)}, u32[]{:S(2)}) %collective-permute-start) | collective-permute-done | bytes 393248 | tf_op jit(solution)/shard_map/while/body/eval_jaxpr/ppermute | solution.py:18
  579.8 10.7 %all_gather.40 = bf16[96,4096]{1,0:T(8,128)(2,1)S(1)} all-gather(bf16[96,2048]{1,0:T(8,128)(2,1)} %get-tuple-element.408), channel_id=1, replica_groups=mesh['dp'=4,'pipe'=4,'tensor'=2] {'tensor'}, dimensions={1}, use_global_device_ids=true | all-gather | bytes 1179648 | tf_op jit(solution)/shard_map/while/body/eval_jaxpr/all_gather | solution.py:38
  590.8 10.4 %fusion.89 = f32[96,3072]{1,0:T(8,128)S(1)} fusion(bf16[4096,3072]{1,0:T(8,128)(2,1)} %get-tuple-element.427, bf16[96,4096]{1,0:T(8,128)(2,1)S(1)} %all_gather.40, f32[4096]{0:T(1024)S(1)} %bitcast.110, f32[96]{0:T(128)S(1)} %add_rsqrt_fusion.3), kind=kOutput, calls=%fused_computation.17.clone.1 | convolution fusion | flops 2417491968 | bytes 27148672 | tf_op jit(solution)/shard_map/while/body/eval_jaxpr/dot_general | solution.py:106
  606.5 9.5 %convolution_convert_fusion.4 = bf16[96,4096]{1,0:T(8,128)(2,1)} fusion(bf16[96,2048]{1,0:T(8,128)(2,1)S(1)} %reshape.355, bf16[2048,4096]{1,0:T(8,128)(2,1)} %get-tuple-element.431), kind=kOutput, calls=%fused_computation.4.clone.1 | convolution fusion | flops 1611005952 | bytes 17956864 | tf_op jit(solution)/shard_map/while/body/eval_jaxpr/dot_general | solution.py:132
  616.0 17.6 %reduce-scatter.5.cloned.1.call-done = bf16[96,2048]{1,0:T(8,128)(2,1)} async-done(((bf16[96,4096]{1,0:T(8,128)(2,1)}), bf16[96,2048]{1,0:T(8,128)(2,1)}) %reduce-scatter.5.cloned.1.call-update) | async-done | bytes 393232 | tf_op jit(solution)/shard_map/while/body/eval_jaxpr/reduce_scatter | solution.py:133
  636.3 9.2 %collective-permute-done = bf16[96,2048]{1,0:T(8,128)(2,1)S(1)} collective-permute-done((bf16[96,2048]{1,0:T(8,128)(2,1)S(1)}, bf16[96,2048]{1,0:T(8,128)(2,1)S(1)}, u32[]{:S(2)}, u32[]{:S(2)}) %collective-permute-start) | collective-permute-done | bytes 393248 | tf_op jit(solution)/shard_map/while/body/eval_jaxpr/ppermute | solution.py:18
  646.3 10.7 %all_gather.40 = bf16[96,4096]{1,0:T(8,128)(2,1)S(1)} all-gather(bf16[96,2048]{1,0:T(8,128)(2,1)} %get-tuple-element.408), channel_id=1, replica_groups=mesh['dp'=4,'pipe'=4,'tensor'=2] {'tensor'}, dimensions={1}, use_global_device_ids=true | all-gather | bytes 1179648 | tf_op jit(solution)/shard_map/while/body/eval_jaxpr/all_gather | solution.py:38
  657.3 10.4 %fusion.89 = f32[96,3072]{1,0:T(8,128)S(1)} fusion(bf16[4096,3072]{1,0:T(8,128)(2,1)} %get-tuple-element.427, bf16[96,4096]{1,0:T(8,128)(2,1)S(1)} %all_gather.40, f32[4096]{0:T(1024)S(1)} %bitcast.110, f32[96]{0:T(128)S(1)} %add_rsqrt_fusion.3), kind=kOutput, calls=%fused_computation.17.clone.1 | convolution fusion | flops 2417491968 | bytes 27148672 | tf_op jit(solution)/shard_map/while/body/eval_jaxpr/dot_general | solution.py:106
  673.0 9.5 %convolution_convert_fusion.4 = bf16[96,4096]{1,0:T(8,128)(2,1)} fusion(bf16[96,2048]{1,0:T(8,128)(2,1)S(1)} %reshape.355, bf16[2048,4096]{1,0:T(8,128)(2,1)} %get-tuple-element.431), kind=kOutput, calls=%fused_computation.4.clone.1 | convolution fusion | flops 1611005952 | bytes 17956864 | tf_op jit(solution)/shard_map/while/body/eval_jaxpr/dot_general | solution.py:132
  682.5 17.6 %reduce-scatter.5.cloned.1.call-done = bf16[96,2048]{1,0:T(8,128)(2,1)} async-done(((bf16[96,4096]{1,0:T(8,128)(2,1)}), bf16[96,2048]{1,0:T(8,128)(2,1)}) %reduce-scatter.5.cloned.1.call-update) | async-done | bytes 393232 | tf_op jit(solution)/shard_map/while/body/eval_jaxpr/reduce_scatter | solution.py:133
  702.8 9.2 %collective-permute-done = bf16[96,2048]{1,0:T(8,128)(2,1)S(1)} collective-permute-done((bf16[96,2048]{1,0:T(8,128)(2,1)S(1)}, bf16[96,2048]{1,0:T(8,128)(2,1)S(1)}, u32[]{:S(2)}, u32[]{:S(2)}) %collective-permute-start) | collective-permute-done | bytes 393248 | tf_op jit(solution)/shard_map/while/body/eval_jaxpr/ppermute | solution.py:18
  712.8 10.8 %all_gather.35 = bf16[96,4096]{1,0:T(8,128)(2,1)S(1)} all-gather(bf16[96,2048]{1,0:T(8,128)(2,1)} %get-tuple-element.268), channel_id=1, replica_groups=mesh['dp'=4,'pipe'=4,'tensor'=2] {'tensor'}, dimensions={1}, use_global_device_ids=true | all-gather | bytes 1179648 | tf_op jit(solution)/shard_map/all_gather | solution.py:38
  725.6 32.5 %psum.14 = bf16[32]{0:T(256)(128)(2,1)S(1)} all-reduce(bf16[32]{0:T(256)(128)(2,1)S(1)} %convert_reduce_fusion), channel_id=1, replica_groups=mesh['dp'=4,'pipe'=4,'tensor'=2] {'dp','pipe'}, use_global_device_ids=true, to_apply=%region_11.12 | all-reduce | flops 32 | bytes 128 | tf_op jit(solution)/shard_map/psum | solution.py:171
  (315 shorter events, 105.6 us)
Async XLA Ops:
  7.2 173.2 %reduce-scatter.3.cloned.1.call-start = ((), (), s32[]{:S(2)}) async-start(), calls=%async_computation.2 | async-start | bytes 6684672 | tf_op jit(solution)/shard_map/reduce_scatter | solution.py:83
  97.3 0.7 copy-start.6
  97.3 2.1 copy-start.5
  108.2 72.1 %copy-start.2 = (f32[1,4096]{1,0:T(1,128)S(1)}, f32[1,4096]{1,0:T(1,128)}, u32[]{:S(2)}) copy-start(f32[1,4096]{1,0:T(1,128)} %param.22) | copy-start | bytes 49156
  180.3 543.7 %dynamic-slice-start = ((f32[4096]{0:T(1024)}, s32[]{:T(128)}), f32[2048]{0:T(1024)S(1)}, s32[]{:S(2)}) async-start(f32[4096]{0:T(1024)} %param.27, s32[]{:T(128)} %select_n.115), calls=%async_computation.5 | async-start | bytes 16896 | tf_op jit(solution)/shard_map/dynamic_slice | solution.py:153
  180.3 54.2 %reduce-scatter.5.cloned.1.call-start = ((), (), s32[]{:S(2)}) async-start(), calls=%async_computation.4 | async-start | bytes 1179648 | tf_op jit(solution)/shard_map/while/body/eval_jaxpr/reduce_scatter | solution.py:133
  207.3 27.2 %copy-start = (bf16[96,2048]{1,0:T(8,128)(2,1)S(1)}, bf16[96,2048]{1,0:T(8,128)(2,1)}, u32[]{:S(2)}) copy-start(bf16[96,2048]{1,0:T(8,128)(2,1)} %get-tuple-element.408) | copy-start | bytes 1179652 | tf_op jit(solution)/shard_map/while
  235.6 10.8 %collective-permute-start = (bf16[96,2048]{1,0:T(8,128)(2,1)S(1)}, bf16[96,2048]{1,0:T(8,128)(2,1)S(1)}, u32[]{:S(2)}, u32[]{:S(2)}) collective-permute-start(bf16[96,2048]{1,0:T(8,128)(2,1)S(1)} %fusion.94), channel_id=1, source_target_pairs={{6,0},{0,2},{2,4},{4,6},{7,1},{1,3},{3,5},{5,7},{14,8},{8,10},{10,... | collective-permute-start | bytes 1179656 | tf_op jit(solution)/shard_map/while/body/eval_jaxpr/ppermute | solution.py:18
  246.4 0.8 copy-start.1
  247.1 53.9 %reduce-scatter.5.cloned.1.call-start = ((), (), s32[]{:S(2)}) async-start(), calls=%async_computation.4 | async-start | bytes 1179648 | tf_op jit(solution)/shard_map/while/body/eval_jaxpr/reduce_scatter | solution.py:133
  273.8 27.2 %copy-start = (bf16[96,2048]{1,0:T(8,128)(2,1)S(1)}, bf16[96,2048]{1,0:T(8,128)(2,1)}, u32[]{:S(2)}) copy-start(bf16[96,2048]{1,0:T(8,128)(2,1)} %get-tuple-element.408) | copy-start | bytes 1179652 | tf_op jit(solution)/shard_map/while
  302.1 10.7 %collective-permute-start = (bf16[96,2048]{1,0:T(8,128)(2,1)S(1)}, bf16[96,2048]{1,0:T(8,128)(2,1)S(1)}, u32[]{:S(2)}, u32[]{:S(2)}) collective-permute-start(bf16[96,2048]{1,0:T(8,128)(2,1)S(1)} %fusion.94), channel_id=1, source_target_pairs={{6,0},{0,2},{2,4},{4,6},{7,1},{1,3},{3,5},{5,7},{14,8},{8,10},{10,... | collective-permute-start | bytes 1179656 | tf_op jit(solution)/shard_map/while/body/eval_jaxpr/ppermute | solution.py:18
  312.9 0.8 copy-start.1
  313.6 53.9 %reduce-scatter.5.cloned.1.call-start = ((), (), s32[]{:S(2)}) async-start(), calls=%async_computation.4 | async-start | bytes 1179648 | tf_op jit(solution)/shard_map/while/body/eval_jaxpr/reduce_scatter | solution.py:133
  340.3 27.3 %copy-start = (bf16[96,2048]{1,0:T(8,128)(2,1)S(1)}, bf16[96,2048]{1,0:T(8,128)(2,1)}, u32[]{:S(2)}) copy-start(bf16[96,2048]{1,0:T(8,128)(2,1)} %get-tuple-element.408) | copy-start | bytes 1179652 | tf_op jit(solution)/shard_map/while
  368.7 10.7 %collective-permute-start = (bf16[96,2048]{1,0:T(8,128)(2,1)S(1)}, bf16[96,2048]{1,0:T(8,128)(2,1)S(1)}, u32[]{:S(2)}, u32[]{:S(2)}) collective-permute-start(bf16[96,2048]{1,0:T(8,128)(2,1)S(1)} %fusion.94), channel_id=1, source_target_pairs={{6,0},{0,2},{2,4},{4,6},{7,1},{1,3},{3,5},{5,7},{14,8},{8,10},{10,... | collective-permute-start | bytes 1179656 | tf_op jit(solution)/shard_map/while/body/eval_jaxpr/ppermute | solution.py:18
  379.4 0.8 copy-start.1
  380.2 53.9 %reduce-scatter.5.cloned.1.call-start = ((), (), s32[]{:S(2)}) async-start(), calls=%async_computation.4 | async-start | bytes 1179648 | tf_op jit(solution)/shard_map/while/body/eval_jaxpr/reduce_scatter | solution.py:133
  406.8 27.2 %copy-start = (bf16[96,2048]{1,0:T(8,128)(2,1)S(1)}, bf16[96,2048]{1,0:T(8,128)(2,1)}, u32[]{:S(2)}) copy-start(bf16[96,2048]{1,0:T(8,128)(2,1)} %get-tuple-element.408) | copy-start | bytes 1179652 | tf_op jit(solution)/shard_map/while
  435.2 10.8 %collective-permute-start = (bf16[96,2048]{1,0:T(8,128)(2,1)S(1)}, bf16[96,2048]{1,0:T(8,128)(2,1)S(1)}, u32[]{:S(2)}, u32[]{:S(2)}) collective-permute-start(bf16[96,2048]{1,0:T(8,128)(2,1)S(1)} %fusion.94), channel_id=1, source_target_pairs={{6,0},{0,2},{2,4},{4,6},{7,1},{1,3},{3,5},{5,7},{14,8},{8,10},{10,... | collective-permute-start | bytes 1179656 | tf_op jit(solution)/shard_map/while/body/eval_jaxpr/ppermute | solution.py:18
  445.9 0.8 copy-start.1
  446.7 53.9 %reduce-scatter.5.cloned.1.call-start = ((), (), s32[]{:S(2)}) async-start(), calls=%async_computation.4 | async-start | bytes 1179648 | tf_op jit(solution)/shard_map/while/body/eval_jaxpr/reduce_scatter | solution.py:133
  473.4 27.2 %copy-start = (bf16[96,2048]{1,0:T(8,128)(2,1)S(1)}, bf16[96,2048]{1,0:T(8,128)(2,1)}, u32[]{:S(2)}) copy-start(bf16[96,2048]{1,0:T(8,128)(2,1)} %get-tuple-element.408) | copy-start | bytes 1179652 | tf_op jit(solution)/shard_map/while
  501.7 10.7 %collective-permute-start = (bf16[96,2048]{1,0:T(8,128)(2,1)S(1)}, bf16[96,2048]{1,0:T(8,128)(2,1)S(1)}, u32[]{:S(2)}, u32[]{:S(2)}) collective-permute-start(bf16[96,2048]{1,0:T(8,128)(2,1)S(1)} %fusion.94), channel_id=1, source_target_pairs={{6,0},{0,2},{2,4},{4,6},{7,1},{1,3},{3,5},{5,7},{14,8},{8,10},{10,... | collective-permute-start | bytes 1179656 | tf_op jit(solution)/shard_map/while/body/eval_jaxpr/ppermute | solution.py:18
  512.5 0.8 copy-start.1
  513.2 53.9 %reduce-scatter.5.cloned.1.call-start = ((), (), s32[]{:S(2)}) async-start(), calls=%async_computation.4 | async-start | bytes 1179648 | tf_op jit(solution)/shard_map/while/body/eval_jaxpr/reduce_scatter | solution.py:133
  539.9 27.2 %copy-start = (bf16[96,2048]{1,0:T(8,128)(2,1)S(1)}, bf16[96,2048]{1,0:T(8,128)(2,1)}, u32[]{:S(2)}) copy-start(bf16[96,2048]{1,0:T(8,128)(2,1)} %get-tuple-element.408) | copy-start | bytes 1179652 | tf_op jit(solution)/shard_map/while
  568.2 10.8 %collective-permute-start = (bf16[96,2048]{1,0:T(8,128)(2,1)S(1)}, bf16[96,2048]{1,0:T(8,128)(2,1)S(1)}, u32[]{:S(2)}, u32[]{:S(2)}) collective-permute-start(bf16[96,2048]{1,0:T(8,128)(2,1)S(1)} %fusion.94), channel_id=1, source_target_pairs={{6,0},{0,2},{2,4},{4,6},{7,1},{1,3},{3,5},{5,7},{14,8},{8,10},{10,... | collective-permute-start | bytes 1179656 | tf_op jit(solution)/shard_map/while/body/eval_jaxpr/ppermute | solution.py:18
  579.0 0.8 copy-start.1
  579.8 53.8 %reduce-scatter.5.cloned.1.call-start = ((), (), s32[]{:S(2)}) async-start(), calls=%async_computation.4 | async-start | bytes 1179648 | tf_op jit(solution)/shard_map/while/body/eval_jaxpr/reduce_scatter | solution.py:133
  606.5 27.2 %copy-start = (bf16[96,2048]{1,0:T(8,128)(2,1)S(1)}, bf16[96,2048]{1,0:T(8,128)(2,1)}, u32[]{:S(2)}) copy-start(bf16[96,2048]{1,0:T(8,128)(2,1)} %get-tuple-element.408) | copy-start | bytes 1179652 | tf_op jit(solution)/shard_map/while
  634.8 10.8 %collective-permute-start = (bf16[96,2048]{1,0:T(8,128)(2,1)S(1)}, bf16[96,2048]{1,0:T(8,128)(2,1)S(1)}, u32[]{:S(2)}, u32[]{:S(2)}) collective-permute-start(bf16[96,2048]{1,0:T(8,128)(2,1)S(1)} %fusion.94), channel_id=1, source_target_pairs={{6,0},{0,2},{2,4},{4,6},{7,1},{1,3},{3,5},{5,7},{14,8},{8,10},{10,... | collective-permute-start | bytes 1179656 | tf_op jit(solution)/shard_map/while/body/eval_jaxpr/ppermute | solution.py:18
  645.5 0.8 copy-start.1
  646.3 53.9 %reduce-scatter.5.cloned.1.call-start = ((), (), s32[]{:S(2)}) async-start(), calls=%async_computation.4 | async-start | bytes 1179648 | tf_op jit(solution)/shard_map/while/body/eval_jaxpr/reduce_scatter | solution.py:133
  673.0 27.2 %copy-start = (bf16[96,2048]{1,0:T(8,128)(2,1)S(1)}, bf16[96,2048]{1,0:T(8,128)(2,1)}, u32[]{:S(2)}) copy-start(bf16[96,2048]{1,0:T(8,128)(2,1)} %get-tuple-element.408) | copy-start | bytes 1179652 | tf_op jit(solution)/shard_map/while
  701.3 10.7 %collective-permute-start = (bf16[96,2048]{1,0:T(8,128)(2,1)S(1)}, bf16[96,2048]{1,0:T(8,128)(2,1)S(1)}, u32[]{:S(2)}, u32[]{:S(2)}) collective-permute-start(bf16[96,2048]{1,0:T(8,128)(2,1)S(1)} %fusion.94), channel_id=1, source_target_pairs={{6,0},{0,2},{2,4},{4,6},{7,1},{1,3},{3,5},{5,7},{14,8},{8,10},{10,... | collective-permute-start | bytes 1179656 | tf_op jit(solution)/shard_map/while/body/eval_jaxpr/ppermute | solution.py:18
  712.0 0.8 copy-start.1
  712.8 11.6 %copy-start.4 = (s32[2,1]{0,1:T(1,128)S(1)}, s32[2,1]{0,1:T(1,128)}, u32[]{:S(2)}) copy-start(s32[2,1]{0,1:T(1,128)} %param.17) | copy-start | bytes 28
  712.8 53.3 %all-gather.5.cloned.1.call-start = ((), (), s32[]{:S(2)}) async-start(), calls=%async_computation.3 | async-start | bytes 2228224 | tf_op jit(solution)/shard_map/all_gather | solution.py:168
  768.1 6.3 copy-start.3
Sparse Core Ops, SparseCore 0:
  97.4 82.8 reduce-scatter.2
  217.0 17.4 reduce-scatter.4
  283.5 17.4 reduce-scatter.4
  350.0 17.5 reduce-scatter.4
  416.5 17.4 reduce-scatter.4
  483.1 17.5 reduce-scatter.4
  549.6 17.4 reduce-scatter.4
  616.1 17.4 reduce-scatter.4
  682.6 17.4 reduce-scatter.4
  725.7 40.3 all-gather.4
